TPU v7x, 32 devices: a whole 2x2x4 slice. The times are simulated.
32 devices in a mesh: prow: 4 (over y, core), pcol: 8 (over z, x).
Axes of the slice: x: 2, y: 2, z: 4, core: 2. Of those that a mesh axis runs over, the one named last changes fastest.
Arguments:
- matrix: bfloat16 [2, 8, 4, 256, 2, 8, 256], P(None, None, 'prow', None, None, 'pcol'), may hold values from -6 to 6
Outputs:
- image: float32 [2, 8, 4, 256, 2, 8, 256], P(None, None, 'prow', None, None, 'pcol')
All inputs are finite; a program needn't handle non-finite values.
Results may differ from a plain program's by a relative error of at most 0.0003.
Values sent between devices are 32-bit elements; how exact they have to be, the bound alone decides.
A program may use at most 64 MiB of HBM per device.

v0:
```python
import jax
import jax.numpy as jnp
from jax import lax
from jax.sharding import PartitionSpec as P

HIGH = lax.Precision.HIGHEST


def prefix(value, axis, combine, identity):
    length, here = (lax.axis_size(axis), lax.axis_index(axis))
    everything = lax.all_gather(value, axis)
    start = jnp.broadcast_to(jnp.asarray(identity, value.dtype), value.shape)

    def lap(k, before):
        reached = k < here
        new = combine(before, everything[k])
        return jnp.where(reached, new, before)

    return lax.fori_loop(0, length, lap, start)


def add_terms(earlier, later):
    return earlier + later


def shards(matrix):
    batch = matrix.shape[0]
    rows_here = matrix.shape[1]
    tile_len = matrix.shape[3]
    cols_here = matrix.shape[4]
    prow_count = lax.axis_size("prow")
    pcol_count = lax.axis_size("pcol")
    prow_index = lax.axis_index("prow")
    pcol_index = lax.axis_index("pcol")
    local = matrix.astype(jnp.float32).reshape(batch, rows_here, tile_len, cols_here, tile_len)
    first_idx = lax.broadcasted_iota(jnp.int32, (tile_len, tile_len), 0)
    second_idx = lax.broadcasted_iota(jnp.int32, (tile_len, tile_len), 1)
    upper = (first_idx <= second_idx).astype(jnp.float32)
    lower = (second_idx <= first_idx).astype(jnp.float32)
    rowscan = jnp.einsum("nrick,kj->nricj", local, upper, precision=HIGH)
    row_sums = rowscan[:, :, :, :, tile_len - 1]
    gathered = lax.all_gather(row_sums, "pcol", axis=3, tiled=True)
    source = jnp.arange(pcol_count * cols_here, dtype=jnp.int32)
    source_glob = source % cols_here * pcol_count + source // cols_here
    target_glob = jnp.arange(cols_here, dtype=jnp.int32) * pcol_count + pcol_index
    earlier_mask = (source_glob[:, None] < target_glob[None, :]).astype(jnp.float32)
    row_carry = jnp.einsum("nrig,gc->nric", gathered, earlier_mask, precision=HIGH)
    rowscan = rowscan + row_carry[:, :, :, :, None]
    colscan = jnp.einsum("ik,nrkcj->nricj", lower, rowscan, precision=HIGH)
    col_sums = colscan[:, :, tile_len - 1, :, :]
    before = prefix(col_sums, "prow", add_terms, jnp.zeros_like(col_sums))
    whole = lax.psum(col_sums, "prow")
    strict = (jnp.arange(rows_here)[:, None] < jnp.arange(rows_here)[None, :]).astype(jnp.float32)
    col_carry = before + jnp.einsum("nscj,sr->nrcj", whole, strict, precision=HIGH)
    colscan = colscan + col_carry[:, :, None, :, :]
    row_glob = (
        jnp.arange(rows_here, dtype=jnp.int32)[:, None] * prow_count + prow_index
    ) * tile_len + jnp.arange(tile_len, dtype=jnp.int32)[None, :]
    col_glob = (
        jnp.arange(cols_here, dtype=jnp.int32)[:, None] * pcol_count + pcol_index
    ) * tile_len + jnp.arange(tile_len, dtype=jnp.int32)[None, :]
    row_factor = 1.0 / jnp.sqrt(row_glob.astype(jnp.float32) + 1.0)
    col_factor = 1.0 / jnp.sqrt(col_glob.astype(jnp.float32) + 1.0)
    scaled = colscan * (row_factor[None, :, :, None, None] * col_factor[None, None, None, :, :])
    return scaled.reshape(batch, rows_here, 1, tile_len, cols_here, 1, tile_len)


def solution(mesh):
    return jax.shard_map(
        shards,
        mesh=mesh,
        in_specs=(P(None, None, "prow", None, None, "pcol", None),),
        out_specs=P(None, None, "prow", None, None, "pcol", None),
        check_vma=False,
    )
```

profile of v0, /device:TPU:0, one launch (start us, length us, event | category | flops | bytes accessed | tf_op | source)
XLA Modules:
  0.0 76.3 jit_solution(13902189001919219110)
XLA Ops:
  0.0 3.5 %fusion.8 = f32[2,8,256,2,256]{2,4,3,1,0:T(8,128)S(1)} fusion(bf16[2,8,256,2,256]{4,3,2,1,0:T(2,128)(2,1)} %bitcast.44), kind=kOutput, calls=%fused_computation.10 | convolution fusion | flops 1073807360 | bytes 12582912 | tf_op jit(solution)/shard_map/nrick,kj->nricj/dot_general | solution.py:40
  3.5 28.3 %all-gather = f32[2,8,256,16,1]{2,4,3,1,0:T(1,128)S(1)} all-gather(f32[2,8,256,2,1]{2,4,3,1,0:T(1,128)S(1)} %slice.8), channel_id=2, replica_groups=mesh['prow'=4,'pcol'=8] {'pcol'}, dimensions={3}, use_global_device_ids=true | all-gather | bytes 294912 | tf_op jit(solution)/shard_map/all_gather | solution.py:42
  31.9 0.3 fusion.12
  32.2 4.9 %fusion.5 = f32[2,8,256,2,256]{4,2,3,1,0:T(8,128)S(1)} fusion(f32[2,8,256,2,256]{2,4,3,1,0:T(8,128)S(1)} %fusion.8, f32[2,8,256,2]{2,3,1,0:T(2,128)S(1)} %fusion.12), kind=kOutput, calls=%fused_computation.9 | convolution fusion | flops 6444613632 | bytes 16809984 | tf_op jit(solution)/shard_map/ik,nrkcj->nricj/dot_general | solution.py:49
  37.2 0.0 copy-start
  37.2 3.4 %copy-done = f32[2,8,256,2,256]{4,2,3,1,0:T(8,128)} copy-done((f32[2,8,256,2,256]{4,2,3,1,0:T(8,128)}, f32[2,8,256,2,256]{4,2,3,1,0:T(8,128)S(1)}, u32[]{:S(2)}) %copy-start) | copy-done | bytes 8388632
  40.6 5.4 %all-gather.1 = f32[8,8,1,2,256]{4,1,3,2,0:T(8,128)S(1)} all-gather(f32[2,8,1,2,256]{4,1,3,2,0:T(8,128)S(1)} %copy.10), channel_id=3, replica_groups=mesh['prow'=4,'pcol'=8] {'prow'}, dimensions={0}, use_global_device_ids=true | all-gather | bytes 163840 | tf_op jit(solution)/shard_map/all_gather | solution.py:11
  46.0 0.3 while.14
  46.3 11.6 %psum.7 = f32[2,8,2,256]{3,2,1,0:T(2,128)S(1)} all-reduce(f32[2,8,2,256]{3,2,1,0:T(2,128)S(1)} %bitcast.46), channel_id=1, replica_groups=mesh['prow'=4,'pcol'=8] {'prow'}, use_global_device_ids=true, to_apply=%region_2.3 | all-reduce | flops 8192 | bytes 65536 | tf_op jit(solution)/shard_map/psum | solution.py:52
  58.0 0.1 fusion.11
  58.1 0.1 add_rsqrt_fusion
  58.2 0.1 add_rsqrt_fusion.1
  58.3 2.3 %broadcast_multiply_fusion = f32[8,256,2,256]{3,1,2,0:T(8,128)} fusion(f32[2,256]{1,0:T(2,128)S(1)} %add_rsqrt_fusion.1, f32[8,256]{1,0:T(8,128)S(1)} %add_rsqrt_fusion), kind=kLoop, calls=%fused_computation.11 | loop fusion | flops 1048576 | bytes 4204544 | tf_op jit(solution)/shard_map/mul | solution.py:64
  60.6 5.8 %multiply_bitcast_fusion = f32[2,8,1,256,2,1,256]{6,3,4,1,0,5,2:T(8,128)S(1)} fusion(f32[2,8,256,2,256]{4,2,3,1,0:T(8,128)} %copy-done, f32[8,256,2,256]{3,1,2,0:T(8,128)} %broadcast_multiply_fusion, f32[2,8,2,256]{3,2,1,0:T(2,128)S(1)} %copy.14), kind=kLoop, calls=%fused_computation.3 | loop fusion | flops 4194304 | bytes 21004288 | tf_op jit(solution)/shard_map/reshape | solution.py:65
  66.4 9.9 %copy.15 = f32[2,8,1,256,2,1,256]{6,5,4,3,2,1,0:T(1,128)} copy(f32[2,8,1,256,2,1,256]{6,3,4,1,0,5,2:T(8,128)S(1)} %multiply_bitcast_fusion) | data formatting | bytes 16777216 | tf_op jit(solution)/shard_map/reshape | solution.py:65
  (18 shorter events, 0.3 us)
Async XLA Ops:
  37.2 3.4 %copy-start = (f32[2,8,256,2,256]{4,2,3,1,0:T(8,128)}, f32[2,8,256,2,256]{4,2,3,1,0:T(8,128)S(1)}, u32[]{:S(2)}) copy-start(f32[2,8,256,2,256]{4,2,3,1,0:T(8,128)S(1)} %fusion.5) | copy-start | bytes 25165828
where the time goes:
time: 76.5 us; the launch traced here: 76.3 us
  blocking collectives  45.4 us (59%)
  local copies, waits for them, and re-layouts  13.4 us (18%)
  matrix products  8.87 us (12%)
  other arithmetic  8.4 us (11%)
    all_gather x1, blocking collectives, shards(): gathered = lax.all_gather(row_sums, 'pcol', axis=3, tiled=True)  28.3 us
    psum x1, blocking collectives, shards(): whole = lax.psum(col_sums, 'prow')  11.6 us
    reshape x1, local copies, waits for them, and re-layouts, shards(): return scaled.reshape(batch, rows_here, 1, tile_len, cols_here, 1, tile_len)  9.91 us
    reshape x1, other arithmetic, shards(): return scaled.reshape(batch, rows_here, 1, tile_len, cols_here, 1, tile_len)  5.81 us
    all_gather x1, blocking collectives, prefix(): everything = lax.all_gather(value, axis)  5.42 us
    dot_general x1, matrix products, shards(): colscan = jnp.einsum('ik,nrkcj->nricj', lower, rowscan, precision=HIGH)  4.93 us
    dot_general x1, matrix products, shards(): rowscan = jnp.einsum('nrick,kj->nricj', local, upper, precision=HIGH)  3.48 us
    unnamed x3, local copies, waits for them, and re-layouts  3.41 us

commit v1 on v0

--- a/solution.py
+++ b/solution.py
@@ -4,6 +4,11 @@
 from jax.sharding import PartitionSpec as P
 
 HIGH = lax.Precision.HIGHEST
+
+
+def summed_here(x, name):
+    pieces = lax.all_gather(x, name)
+    return jnp.sum(pieces, axis=0)
 
 
 def prefix(value, axis, combine, identity):
@@ -49,7 +54,7 @@
     colscan = jnp.einsum("ik,nrkcj->nricj", lower, rowscan, precision=HIGH)
     col_sums = colscan[:, :, tile_len - 1, :, :]
     before = prefix(col_sums, "prow", add_terms, jnp.zeros_like(col_sums))
-    whole = lax.psum(col_sums, "prow")
+    whole = summed_here(col_sums, "prow")
     strict = (jnp.arange(rows_here)[:, None] < jnp.arange(rows_here)[None, :]).astype(jnp.float32)
     col_carry = before + jnp.einsum("nscj,sr->nrcj", whole, strict, precision=HIGH)
     colscan = colscan + col_carry[:, :, None, :, :]

time: 76.5 us -> 64.8 us (0.85)
  blocking collectives: 45.4 us -> 33.8 us
    psum x1 -> x0, blocking collectives: 11.6 us -> none  [shards(): whole = lax.psum(col_sums, 'prow')]
    unnamed x3 -> x2, local copies, waits for them, and re-layouts: 3.41 us -> 3.39 us
where the time goes in v1:
time: 64.8 us; the launch traced here: 64.7 us
  blocking collectives  33.8 us (52%)
  local copies, waits for them, and re-layouts  13.4 us (21%)
  matrix products  8.87 us (14%)
  other arithmetic  8.42 us (13%)
    all_gather x1, blocking collectives, shards(): gathered = lax.all_gather(row_sums, 'pcol', axis=3, tiled=True)  28.3 us
    reshape x1, local copies, waits for them, and re-layouts, shards(): return scaled.reshape(batch, rows_here, 1, tile_len, cols_here, 1, tile_len)  9.91 us
    reshape x1, other arithmetic, shards(): return scaled.reshape(batch, rows_here, 1, tile_len, cols_here, 1, tile_len)  5.81 us
    all_gather x1, blocking collectives, prefix(): everything = lax.all_gather(value, axis)  5.42 us
    dot_general x1, matrix products, shards(): colscan = jnp.einsum('ik,nrkcj->nricj', lower, rowscan, precision=HIGH)  4.93 us
    dot_general x1, matrix products, shards(): rowscan = jnp.einsum('nrick,kj->nricj', local, upper, precision=HIGH)  3.48 us
    unnamed x2, local copies, waits for them, and re-layouts  3.39 us
    mul x1, other arithmetic, shards(): row_factor[None, :, :, None, None] * col_factor[None, None, None, :, :]  2.27 us

profile of v1, /device:TPU:0, one launch (start us, length us, event | category | flops | bytes accessed | tf_op | source)
XLA Modules:
  0.0 64.7 jit_solution(12529521909542212022)
XLA Ops:
  0.0 3.5 %fusion.8 = f32[2,8,256,2,256]{2,4,3,1,0:T(8,128)S(1)} fusion(bf16[2,8,256,2,256]{4,3,2,1,0:T(2,128)(2,1)} %bitcast.42), kind=kOutput, calls=%fused_computation.10 | convolution fusion | flops 1073807360 | bytes 12582912 | tf_op jit(solution)/shard_map/nrick,kj->nricj/dot_general | solution.py:45
  3.5 28.3 %all-gather = f32[2,8,256,16,1]{2,4,3,1,0:T(1,128)S(1)} all-gather(f32[2,8,256,2,1]{2,4,3,1,0:T(1,128)S(1)} %slice.8), channel_id=2, replica_groups=mesh['prow'=4,'pcol'=8] {'pcol'}, dimensions={3}, use_global_device_ids=true | all-gather | bytes 294912 | tf_op jit(solution)/shard_map/all_gather | solution.py:47
  31.9 0.3 fusion.12
  32.2 4.9 %fusion.5 = f32[2,8,256,2,256]{4,2,3,1,0:T(8,128)S(1)} fusion(f32[2,8,256,2,256]{2,4,3,1,0:T(8,128)S(1)} %fusion.8, f32[2,8,256,2]{2,3,1,0:T(2,128)S(1)} %fusion.12), kind=kOutput, calls=%fused_computation.9 | convolution fusion | flops 6444613632 | bytes 16809984 | tf_op jit(solution)/shard_map/ik,nrkcj->nricj/dot_general | solution.py:54
  37.2 0.0 copy-start
  37.2 3.4 %copy-done = f32[2,8,256,2,256]{4,2,3,1,0:T(8,128)} copy-done((f32[2,8,256,2,256]{4,2,3,1,0:T(8,128)}, f32[2,8,256,2,256]{4,2,3,1,0:T(8,128)S(1)}, u32[]{:S(2)}) %copy-start) | copy-done | bytes 8388632
  40.6 5.4 %all-gather.1 = f32[8,8,1,2,256]{4,1,3,2,0:T(8,128)S(1)} all-gather(f32[2,8,1,2,256]{4,1,3,2,0:T(8,128)S(1)} %copy.9), channel_id=3, replica_groups=mesh['prow'=4,'pcol'=8] {'prow'}, dimensions={0}, use_global_device_ids=true | all-gather | bytes 163840 | tf_op jit(solution)/shard_map/all_gather | solution.py:16
  46.0 0.3 while.14
  46.3 0.1 fusion.11
  46.5 0.1 add_rsqrt_fusion
  46.6 0.1 add_rsqrt_fusion.1
  46.7 2.3 %broadcast_multiply_fusion = f32[8,256,2,256]{3,1,2,0:T(8,128)} fusion(f32[2,256]{1,0:T(2,128)S(1)} %add_rsqrt_fusion.1, f32[8,256]{1,0:T(8,128)S(1)} %add_rsqrt_fusion), kind=kLoop, calls=%fused_computation.11 | loop fusion | flops 1048576 | bytes 4204544 | tf_op jit(solution)/shard_map/mul | solution.py:69
  48.9 5.8 %multiply_bitcast_fusion = f32[2,8,1,256,2,1,256]{6,3,4,1,0,5,2:T(8,128)S(1)} fusion(f32[2,8,256,2,256]{4,2,3,1,0:T(8,128)} %copy-done, f32[8,256,2,256]{3,1,2,0:T(8,128)} %broadcast_multiply_fusion, f32[2,8,2,256]{3,2,1,0:T(2,128)S(1)} %copy.14), kind=kLoop, calls=%fused_computation.3 | loop fusion | flops 4194304 | bytes 21004288 | tf_op jit(solution)/shard_map/reshape | solution.py:70
  54.8 9.9 %copy.15 = f32[2,8,1,256,2,1,256]{6,5,4,3,2,1,0:T(1,128)} copy(f32[2,8,1,256,2,1,256]{6,3,4,1,0,5,2:T(8,128)S(1)} %multiply_bitcast_fusion) | data formatting | bytes 16777216 | tf_op jit(solution)/shard_map/reshape | solution.py:70
  (18 shorter events, 0.3 us)
Async XLA Ops:
  37.2 3.4 %copy-start = (f32[2,8,256,2,256]{4,2,3,1,0:T(8,128)}, f32[2,8,256,2,256]{4,2,3,1,0:T(8,128)S(1)}, u32[]{:S(2)}) copy-start(f32[2,8,256,2,256]{4,2,3,1,0:T(8,128)S(1)} %fusion.5) | copy-start | bytes 25165828
